TPU v7x, 512 devices: a whole 4x4x16 slice. The times are simulated.
512 devices in a mesh: sample: 4 (over y), row: 8 (over x, core), col: 16 (over z).
Axes of the slice: x: 4, y: 4, z: 16, core: 2. Of those that a mesh axis runs over, the one named last changes fastest.
Arguments:
- pair: bfloat16 [3584, 896, 128], P(('sample', 'row'), 'col'), parts along dimension 0, may hold values from -6 to 6
- pair_gain: float32 [128], replicated, may hold values from 0.1 to 1.9
- bias_weight: bfloat16 [128, 16], replicated, may hold values from -0.5 to 0.5
- single: bfloat16 [3584, 384], P(('sample', 'row', 'col')), parts along dimension 0, may hold values from -50 to 50
- w_query: bfloat16 [384, 384], replicated, may hold values from -0.30618622 to 0.30618622
- w_key: bfloat16 [384, 384], replicated, may hold values from -0.30618622 to 0.30618622
- w_value: bfloat16 [384, 384], replicated, may hold values from -0.3125 to 0.3125
- w_out: bfloat16 [384, 384], replicated, may hold values from -0.3125 to 0.3125
- key_mask: int32 [3584], P(('sample', 'col')), parts along dimension 0, may hold values from 0 to 1, as said below
- out_grad: bfloat16 [3584, 384], P(('sample', 'row', 'col')), parts along dimension 0, may hold values from -6 to 6
Outputs:
- pair_grad: bfloat16 [3584, 896, 128], P(('sample', 'row'), 'col'), parts along dimension 0
- single_grad: bfloat16 [3584, 384], P(('sample', 'row', 'col')), parts along dimension 0
- query_weight_grad: float32 [1536, 384], P(('sample', 'row', 'col')), parts along dimension 0
- key_weight_grad: float32 [1536, 384], P(('sample', 'row', 'col')), parts along dimension 0
- value_weight_grad: float32 [1536, 384], P(('sample', 'row', 'col')), parts along dimension 0
- out_weight_grad: float32 [1536, 384], P(('sample', 'row', 'col')), parts along dimension 0
- bias_weight_grad: float32 [512, 16], P('sample'), parts along dimension 0
- gain_grad: float32 [512], P('sample'), parts along dimension 0
There are 4 independent parts, one for each index of `sample`. A program takes and returns all parts, laid end to end along the dimension named above; an argument that names none is the same for every part. Nothing has to cross between parts.
Inputs may be any that keep to these rules, and one draw needn't show every extreme that they name: key_mask is 1 exactly on a prefix of the tokens whose length is a multiple of 4, at least half of 896 and at most 892, and 0 after it.
All inputs are finite; a program needn't handle non-finite values.
Results may differ from a plain program's by a relative error of at most 0.04.
Values may be sent and summed in bfloat16 or wider, within the bound.
No kernel may reach another device: no remote copies, remote signals or barrier semaphores. Data moves between devices by JAX's collectives and lax.ppermute only.
A program may use at most 64 MiB of HBM per device.

v0:
```python
import functools
import jax
import jax.numpy as jnp
from jax import lax
from jax.sharding import Mesh
from jax.sharding import PartitionSpec as P

HEADS = 16
HEAD = 24
ROW = ("row_0", "row_1")
ROW_COL = ("row_0", "row_1", "col")
SAMPLE_ROW = ("sample", "row_0", "row_1")
SAMPLE_ROW_COL = ("sample", "row_0", "row_1", "col")
norm_eps = 1e-05
masked_score = -1000000000.0
highest = lax.Precision.HIGHEST


def laid_out(pieces, dim):
    shape = list(pieces.shape[1:])
    shape[dim] *= pieces.shape[0]
    return jnp.moveaxis(pieces, 0, dim).reshape(shape)


def stacked_from(array, axes, sequence):
    pieces = array[None]
    for k in sequence:
        pieces = lax.all_gather(pieces, axes[k], axis=0, tiled=True)
    carried = [lax.axis_size(axes[k]) for k in reversed(sequence)]
    pieces = pieces.reshape(*carried, *array.shape)
    turned = sorted(range(len(sequence)), key=lambda place: sequence[len(sequence) - 1 - place])
    return pieces.transpose(*turned, *range(len(sequence), pieces.ndim)).reshape(-1, *array.shape)


def gather_axes(array, axes, sequence, dim):
    return laid_out(stacked_from(array, axes, sequence), dim)


def from_everyone(array, axis):
    devices = lax.axis_size(axis)
    return lax.all_to_all(
        jnp.broadcast_to(array[None], (devices, *array.shape)), axis, 0, 0, tiled=True
    )


def gather_directly(array, axis, dim):
    pieces = from_everyone(array, axis)
    return laid_out(pieces, dim)


def collected_together(array, axis):
    leaves = jax.tree.leaves(array)
    sequence = sorted(range(len(leaves)), key=lambda k: -leaves[k].size)
    width = (1, *leaves[sequence[0]].shape)[-1]
    lines = [
        jnp.pad(leaves[k].reshape(-1), (0, -leaves[k].size % width)).reshape(-1, width)
        for k in sequence
    ]
    both, at, found = (from_everyone(jnp.concatenate(lines), axis), 0, {})
    for k, line in zip(sequence, lines):
        slab = both[:, at : at + len(line)].reshape(len(both), -1)
        found[k] = slab[:, : leaves[k].size].reshape(-1, *leaves[k].shape)
        at += len(line)
    numbers = iter(range(len(leaves)))
    return jax.tree.map(lambda _: found[next(numbers)], array)


def joined_by_halves(pieces, combine):
    while len(jax.tree.leaves(pieces)[0]) > 1:
        pieces = jax.vmap(combine)(
            *(jax.tree.map(lambda part: part[side::2], pieces) for side in (0, 1))
        )
    return jax.tree.map(lambda part: part[0], pieces)


def joined_all(array, axis, combine):
    pieces = collected_together(array, axis)
    return joined_by_halves(pieces, combine)


def over_pieces(array, axis):
    pieces = lax.all_gather(array, axis)
    return pieces.sum(axis=0)


def over_axes(array, axes):
    return functools.reduce(lax.psum, axes, array)


def taken_together(array, axis):
    everything = from_everyone(array, axis)
    return jnp.sum(everything.astype(jnp.float32), axis=0)


def broadcast(array, axis, root):
    return lax.dynamic_index_in_dim(lax.all_gather(array, axis), root, 0, keepdims=False)


def split_up(array, dim, devices):
    before, after = (array.shape[:dim], array.shape[dim + 1 :])
    return jnp.moveaxis(array.reshape(*before, devices, -1, *after), dim, 0)


def sum_at_owner(array, axis, dim):
    devices = lax.axis_size(axis)
    pieces = lax.all_to_all(split_up(array, dim, devices), axis, 0, 0, tiled=True)
    return jnp.sum(pieces.astype(jnp.float32), axis=0)


def sent_together(arrays, axis, dim, along):
    widths = [a.shape[along] for a in arrays]
    both = jnp.concatenate(arrays, axis=along)
    filled = sum_at_owner(both, axis, dim)
    return tuple(jnp.split(filled, [sum(widths[:k]) for k in range(1, len(widths))], axis=along))


def combine_stats(first, second):
    joint_top = jnp.maximum(first[0], second[0])
    joint_total = first[1] * jnp.exp(first[0] - joint_top) + second[1] * jnp.exp(
        second[0] - joint_top
    )
    return (joint_top, joint_total)


def project(grads, weight):
    return jnp.dot(grads, weight.astype(jnp.float32).T, precision=highest)


def transposed_product(left, right):
    return jnp.einsum("te,td->ed", left.astype(jnp.float32), right, precision=highest)


def body(pair, pair_gain, bias_weight, single, w_query, w_key, w_value, w_out, key_mask, out_grad):
    f32 = jnp.float32
    bf16 = jnp.bfloat16
    row_count = pair.shape[0]
    col_count = pair.shape[1]
    own_count = single.shape[0]
    model_width = single.shape[1]
    rows_total = lax.axis_size(ROW)
    cols_total = lax.axis_size("col")
    row_index = lax.axis_index(ROW)
    col_index = lax.axis_index("col")
    score_scale = HEAD ** (-0.5)
    all_single = gather_axes(single, ROW_COL, (2, 0, 1), 0)
    single_rows = lax.dynamic_slice_in_dim(all_single, row_index * row_count, row_count, 0)
    single_cols = lax.dynamic_slice_in_dim(all_single, col_index * col_count, col_count, 0)
    grad_rows = gather_directly(out_grad, "col", 0)
    query_rows = jnp.dot(single_rows, w_query, preferred_element_type=f32).astype(bf16)
    key_cols = jnp.dot(single_cols, w_key, preferred_element_type=f32).astype(bf16)
    value_cols = jnp.dot(single_cols, w_value, preferred_element_type=f32).astype(bf16)
    pair_float = pair.astype(f32)
    centred = pair_float - jnp.mean(pair_float, axis=2, keepdims=True)
    inverse = lax.rsqrt(jnp.mean(centred * centred, axis=2, keepdims=True) + norm_eps)
    normed = centred * inverse
    pair_normed = (normed * pair_gain).astype(bf16)
    pair_bias = jnp.einsum("ijc,ch->hij", pair_normed, bias_weight, preferred_element_type=f32)
    query_heads = query_rows.reshape(row_count, HEADS, HEAD)
    key_heads = key_cols.reshape(col_count, HEADS, HEAD)
    value_heads = value_cols.reshape(col_count, HEADS, HEAD)
    scores = (
        jnp.einsum("ihd,jhd->hij", query_heads, key_heads, preferred_element_type=f32) * score_scale
        + pair_bias
    )
    scores = jnp.where(key_mask[None, None, :] > 0, scores, masked_score)
    local_top = jnp.max(scores, axis=2)
    local_exp = jnp.exp(scores - local_top[:, :, None])
    row_top, row_total = joined_all((local_top, jnp.sum(local_exp, axis=2)), "col", combine_stats)
    exp_scores = local_exp * jnp.exp(local_top - row_top)[:, :, None]
    probs = exp_scores / row_total[:, :, None]
    probs_low = probs.astype(bf16)
    attended_part = jnp.einsum(
        "hij,jhd->ihd", probs_low, value_heads, preferred_element_type=f32
    ).reshape(row_count, model_width)
    attended = over_pieces(attended_part, "col")
    attended_low = attended.astype(bf16)
    grad_att = jnp.dot(grad_rows, w_out.T, preferred_element_type=f32).astype(bf16)
    grad_heads = grad_att.reshape(row_count, HEADS, HEAD)
    grad_probs = jnp.einsum("ihd,jhd->hij", grad_heads, value_heads, preferred_element_type=f32)
    row_delta = jnp.einsum(
        "ihd,ihd->hi", grad_heads.astype(f32), attended.reshape(row_count, HEADS, HEAD)
    )
    grad_scores = probs * (grad_probs - row_delta[:, :, None])
    grad_low = grad_scores.astype(bf16)
    query_grad = (
        jnp.einsum("hij,jhd->ihd", grad_low, key_heads, preferred_element_type=f32) * score_scale
    ).reshape(row_count, model_width)
    key_grad = (
        jnp.einsum("hij,ihd->jhd", grad_low, query_heads, preferred_element_type=f32) * score_scale
    ).reshape(col_count, model_width)
    value_grad = jnp.einsum(
        "hij,ihd->jhd", probs_low, grad_heads, preferred_element_type=f32
    ).reshape(col_count, model_width)
    grad_normed = jnp.einsum("hij,ch->ijc", grad_low, bias_weight, preferred_element_type=f32)
    bias_grad_part = jnp.einsum("ijc,hij->ch", pair_normed, grad_low, preferred_element_type=f32)
    gain_grad_part = jnp.sum(grad_normed * normed, axis=(0, 1))
    bias_weight_grad, gain_grad = (
        over_axes(bias_grad_part, ROW_COL),
        over_axes(gain_grad_part, ROW_COL),
    )
    scaled = grad_normed * pair_gain
    pair_grad = (
        inverse
        * (
            scaled
            - jnp.mean(scaled, axis=2, keepdims=True)
            - normed * jnp.mean(scaled * normed, axis=2, keepdims=True)
        )
    ).astype(bf16)
    own_start = col_index * own_count
    query_sum = taken_together(query_grad.astype(jnp.bfloat16), "col").astype(jnp.float32)
    key_sum, value_sum = (
        taken_together(key_grad.astype(jnp.bfloat16), ROW).astype(jnp.float32),
        taken_together(value_grad.astype(jnp.bfloat16), ROW).astype(jnp.float32),
    )
    own_query = lax.dynamic_slice_in_dim(query_sum, own_start, own_count, 0)
    own_part = project(own_query, w_query)
    key_side = project(key_sum, w_key) + project(value_sum, w_value)
    spread = cols_total // rows_total
    token_start = (row_index * cols_total + col_index) * own_count
    own_root = token_start // col_count
    offset = token_start - own_root * col_count
    for branch in range(spread):
        root_col = row_index * spread + branch
        fetched = broadcast(key_side.astype(jnp.bfloat16), "col", root_col).astype(key_side.dtype)
        piece = lax.dynamic_slice_in_dim(fetched, offset, own_count, 0)
        own_part = own_part + jnp.where(own_root == root_col, piece, 0.0)
    single_grad = own_part.astype(bf16)
    rows_each = model_width // (rows_total * cols_total)
    picked = lax.dynamic_index_in_dim(
        single_rows.reshape(row_count, rows_total, cols_total, rows_each),
        col_index,
        2,
        keepdims=False,
    ).reshape(row_count, rows_total * rows_each)
    att_picked = lax.dynamic_index_in_dim(
        attended_low.reshape(row_count, rows_total, cols_total, rows_each),
        col_index,
        2,
        keepdims=False,
    ).reshape(row_count, rows_total * rows_each)
    query_terms = transposed_product(picked, query_sum)
    out_terms = jnp.einsum("te,td->ed", att_picked, grad_rows, preferred_element_type=f32)
    query_weight_grad, out_weight_grad = sent_together(
        (query_terms.astype(jnp.bfloat16), out_terms.astype(jnp.bfloat16)), ROW, 0, 1
    )
    col_slab = lax.dynamic_slice_in_dim(
        single_cols, row_index * cols_total * rows_each, cols_total * rows_each, 1
    )
    key_weight_grad, value_weight_grad = sent_together(
        (
            transposed_product(col_slab, key_sum).astype(jnp.bfloat16),
            transposed_product(col_slab, value_sum).astype(jnp.bfloat16),
        ),
        "col",
        0,
        1,
    )
    return (
        pair_grad,
        single_grad,
        query_weight_grad,
        key_weight_grad,
        value_weight_grad,
        out_weight_grad,
        bias_weight_grad,
        gain_grad,
    )


def solution(mesh):
    split = Mesh(
        mesh.devices.reshape(mesh.shape["sample"], 4, 2, mesh.shape["col"]),
        ("sample", "row_0", "row_1", "col"),
    )
    placed = (
        P(SAMPLE_ROW, "col", None),
        P(),
        P(),
        P(SAMPLE_ROW_COL, None),
        P(),
        P(),
        P(),
        P(),
        P(("sample", "col")),
        P(SAMPLE_ROW_COL, None),
    )
    return jax.shard_map(
        body,
        mesh=split,
        in_specs=placed,
        out_specs=(
            P(SAMPLE_ROW, "col", None),
            P(SAMPLE_ROW_COL, None),
            P(SAMPLE_ROW_COL, None),
            P(SAMPLE_ROW_COL, None),
            P(SAMPLE_ROW_COL, None),
            P(SAMPLE_ROW_COL, None),
            P("sample", None),
            P("sample"),
        ),
        check_vma=False,
    )
```

profile of v0, /device:TPU:1, one launch (start us, length us, event | category | flops | bytes accessed | tf_op | source)
XLA Modules:
  0.0 361.2 jit_solution(5775855662982069744)
XLA Ops:
  13.4 29.8 %all-gather.2 = bf16[16,7,384]{2,1,0:T(8,128)(2,1)S(1)} all-gather(bf16[1,7,384]{2,1,0:T(8,128)(2,1)S(1)} %bitcast.105), channel_id=2, replica_groups=mesh['sample'=4,'row_0'=4,'row_1'=2,'col'=16] {'col'}, dimensions={0}, use_global_device_ids=true | all-gather | bytes 91392 | tf_op jit(solution)/shard_map/all_gather | solution.py:28
  43.2 9.9 %all_gather.21 = bf16[64,7,384]{2,0,1:T(8,128)(2,1)S(1)} all-gather(bf16[16,7,384]{2,0,1:T(8,128)(2,1)S(1)} %copy.76), channel_id=1, replica_groups=mesh['sample'=4,'row_0'=4,'row_1'=2,'col'=16] {'row_0'}, dimensions={0}, use_global_device_ids=true | all-gather | bytes 430080 | tf_op jit(solution)/shard_map/all_gather | solution.py:28
  53.1 12.5 %all_gather.22 = bf16[128,7,384]{2,0,1:T(8,128)(2,1)S(1)} all-gather(bf16[64,7,384]{2,0,1:T(8,128)(2,1)S(1)} %all_gather.21), channel_id=1, replica_groups=mesh['sample'=4,'row_0'=4,'row_1'=2,'col'=16] {'row_1'}, dimensions={0}, use_global_device_ids=true | all-gather | bytes 1032192 | tf_op jit(solution)/shard_map/all_gather | solution.py:28
  69.6 3.3 fusion.23
  75.7 6.4 %all-to-all-start = ((f32[16,32,112]{2,1,0:T(8,128)}), f32[16,32,112]{2,1,0:T(8,128)S(1)}, u32[]{:S(2)}, u32[]{:S(2)}) async-start(f32[16,32,112]{2,1,0:T(8,128)} %broadcast_in_dim.31), calls=%async_computation | async-start | bytes 524288 | tf_op jit(solution)/shard_map/all_to_all | solution.py:41
  83.3 12.8 %all-to-all-done = f32[16,32,112]{2,1,0:T(8,128)S(1)} async-done(((f32[16,32,112]{2,1,0:T(8,128)}), f32[16,32,112]{2,1,0:T(8,128)S(1)}, u32[]{:S(2)}, u32[]{:S(2)}) %all-to-all-start) | async-done | bytes 229408 | tf_op jit(solution)/shard_map/all_to_all | solution.py:41
  98.0 10.2 %all-to-all-start.1 = ((bf16[16,7,384]{2,1,0:T(8,128)(2,1)}), bf16[16,7,384]{2,1,0:T(8,128)(2,1)S(1)}, u32[]{:S(2)}, u32[]{:S(2)}) async-start(bf16[16,7,384]{2,1,0:T(8,128)(2,1)} %broadcast_in_dim.32), calls=%async_computation.1 | async-start | bytes 196608 | tf_op jit(solution)/shard_map/all_to_all | solution.py:41
  108.2 12.0 %all-to-all-done.1 = bf16[16,7,384]{2,1,0:T(8,128)(2,1)S(1)} async-done(((bf16[16,7,384]{2,1,0:T(8,128)(2,1)}), bf16[16,7,384]{2,1,0:T(8,128)(2,1)S(1)}, u32[]{:S(2)}, u32[]{:S(2)}) %all-to-all-start.1) | async-done | bytes 86048 | tf_op jit(solution)/shard_map/all_to_all | solution.py:41
  122.8 6.4 %all-to-all-start.4 = ((bf16[8,56,384]{2,1,0:T(8,128)(2,1)}), bf16[8,56,384]{2,1,0:T(8,128)(2,1)S(1)}, u32[]{:S(2)}, u32[]{:S(2)}) async-start(bf16[8,56,384]{2,1,0:T(8,128)(2,1)} %broadcast_in_dim.35), calls=%async_computation.4 | async-start | bytes 688128 | tf_op jit(solution)/shard_map/all_to_all | solution.py:41
  129.3 33.4 %all-gather.5.cloned.1.call-done = f32[16,112,384]{2,1,0:T(8,128)} async-done(((f32[1,112,384]{2,1,0:T(8,128)}), f32[16,112,384]{2,1,0:T(8,128)}) %all-gather.5.cloned.1.call-update) | async-done | bytes 2752528 | tf_op jit(solution)/shard_map/all_gather | solution.py:82
  167.1 13.5 %all-to-all-start.3 = ((bf16[8,56,384]{2,1,0:T(8,128)(2,1)}), bf16[8,56,384]{2,1,0:T(8,128)(2,1)S(1)}, u32[]{:S(2)}, u32[]{:S(2)}) async-start(bf16[8,56,384]{2,1,0:T(8,128)(2,1)} %broadcast_in_dim.34), calls=%async_computation.3 | async-start | bytes 688128 | tf_op jit(solution)/shard_map/all_to_all | solution.py:41
  181.8 6.1 %all-to-all-done.3 = bf16[8,56,384]{2,1,0:T(8,128)(2,1)S(1)} async-done(((bf16[8,56,384]{2,1,0:T(8,128)(2,1)}), bf16[8,56,384]{2,1,0:T(8,128)(2,1)S(1)}, u32[]{:S(2)}, u32[]{:S(2)}) %all-to-all-start.3) | async-done | bytes 344096 | tf_op jit(solution)/shard_map/all_to_all | solution.py:41
  189.7 7.4 %all-to-all-start.6 = ((bf16[16,3,768]{2,1,0:T(4,128)(2,1)}), bf16[16,3,768]{2,1,0:T(4,128)(2,1)S(1)}, u32[]{:S(2)}, u32[]{:S(2)}) async-start(bf16[16,3,768]{2,1,0:T(4,128)(2,1)} %reshape.139), calls=%async_computation.6 | async-start | bytes 196608 | tf_op jit(solution)/shard_map/all_to_all | solution.py:106
  198.3 10.6 %all-to-all-done.6 = bf16[16,3,768]{2,1,0:T(4,128)(2,1)S(1)} async-done(((bf16[16,3,768]{2,1,0:T(4,128)(2,1)}), bf16[16,3,768]{2,1,0:T(4,128)(2,1)S(1)}, u32[]{:S(2)}, u32[]{:S(2)}) %all-to-all-start.6) | async-done | bytes 73760 | tf_op jit(solution)/shard_map/all_to_all | solution.py:106
  210.2 4.6 %all-to-all-start.2 = ((bf16[16,112,384]{2,1,0:T(8,128)(2,1)}), bf16[16,112,384]{2,1,0:T(8,128)(2,1)S(1)}, u32[]{:S(2)}, u32[]{:S(2)}) async-start(bf16[16,112,384]{2,1,0:T(8,128)(2,1)} %broadcast_in_dim.33), calls=%async_computation.2 | async-start | bytes 2752512 | tf_op jit(solution)/shard_map/all_to_all | solution.py:41
  225.1 3.8 %convolution_bitcast_fusion = f32[128,16]{0,1:T(8,128)S(1)} fusion(bf16[16,112,56]{2,0,1:T(8,128)(2,1)} %copy.85, bf16[112,56,128]{2,1,0:T(8,128)(2,1)S(1)} %copy-done.1, f32[128]{0:T(128)S(1)} %copy-done.28, f32[112,56]{1,0:T(8,128)} %copy-done.22, f32[112,56]{1,0:T(8,128)} %copy-done.17), kind=kOutput, calls=%fused_computation.41 | convolution fusion | flops 29704192 | bytes 1865216 | tf_op jit(solution)/shard_map/ijc,hij->ch/dot_general | solution.py:195
  229.0 6.4 %fusion.11 = (f32[128]{0:T(128)S(1)}, f32[112,56]{1,0:T(8,128)S(1)}, f32[112,56]{1,0:T(8,128)}, f32[112,56,128]{2,1,0:T(8,128)}) fusion(bf16[112,56,128]{2,1,0:T(8,128)(2,1)S(1)} %copy-done.1, f32[112,56]{1,0:T(8,128)S(1)} %copy-done.23, f32[112,56]{1,0:T(8,128)S(1)} %copy-done.18, f32[128]{0:T(128)} %param.11, bf16[16,112,56]{2,0,1:T(8,128)(2,1)S(1)} %copy-done.19, ...), kind=kOutput, calls=%fused_computation.13 | convolution fusion | flops 32902784 | bytes 5123072 | tf_op jit(solution)/shard_map/hij,ch->ijc/dot_general | solution.py:194
  235.4 8.1 %all-reduce.1 = (f32[128,16]{0,1:T(8,128)S(1)}, f32[128]{0:T(128)}) all-reduce(f32[128,16]{0,1:T(8,128)S(1)} %convolution_bitcast_fusion, f32[128]{0:T(128)S(1)} %get-tuple-element.8), channel_id=1, replica_groups=mesh['sample'=4,'row_0'=4,'row_1'=2,'col'=16] {'row_0'}, use_global_device_ids=true, to_apply=%region_12.13 | all-reduce | flops 2176 | bytes 17408 | tf_op jit(solution)/shard_map/psum | solution.py:87
  243.6 5.9 %all-reduce.2 = (f32[128,16]{0,1:T(8,128)S(1)}, f32[128]{0:T(128)S(1)}) all-reduce(f32[128,16]{0,1:T(8,128)S(1)} %get-tuple-element.13, f32[128]{0:T(128)} %get-tuple-element.14), channel_id=1, replica_groups=mesh['sample'=4,'row_0'=4,'row_1'=2,'col'=16] {'row_1'}, use_global_device_ids=true, to_apply=%region_13.14 | all-reduce | flops 2176 | bytes 17408 | tf_op jit(solution)/shard_map/psum | solution.py:87
  249.4 46.0 %all-reduce = (f32[128,16]{0,1:T(8,128)}, f32[128]{0:T(128)}) all-reduce(f32[128,16]{0,1:T(8,128)S(1)} %get-tuple-element.15, f32[128]{0:T(128)S(1)} %get-tuple-element.16), channel_id=1, replica_groups=mesh['sample'=4,'row_0'=4,'row_1'=2,'col'=16] {'col'}, use_global_device_ids=true, to_apply=%region_14.15 | all-reduce | flops 2176 | bytes 17408 | tf_op jit(solution)/shard_map/psum | solution.py:87
  297.2 7.7 %fusion.10 = bf16[112,56,128]{2,1,0:T(8,128)(2,1)} fusion(bf16[112,56,128]{2,1,0:T(8,128)(2,1)S(1)} %copy-done.1, f32[112,56,128]{2,1,0:T(8,128)} %get-tuple-element.31, f32[112,56]{1,0:T(8,128)S(1)} %get-tuple-element.32, f32[112,56]{1,0:T(8,128)S(1)} %get-tuple-element.33, f32[128]{0:T(128)} %param.11, f32[112,56]{1,0:T(8,128)S(1)} %copy-done.23, ...), kind=kLoop, calls=%fused_computation.12 | loop fusion | flops 7225344 | bytes 6523392 | tf_op jit(solution)/shard_map/convert_element_type | solution.py:209
  305.8 24.5 %all-gather.1 = bf16[896,384]{1,0:T(8,128)(2,1)S(1)} all-gather(bf16[56,384]{1,0:T(8,128)(2,1)S(1)} %fusion.19), channel_id=3, replica_groups=mesh['sample'=4,'row_0'=4,'row_1'=2,'col'=16] {'col'}, dimensions={0}, use_global_device_ids=true | all-gather | bytes 731136 | tf_op jit(solution)/shard_map/all_gather | solution.py:96
  332.0 16.9 %all-to-all-start.5 = ((bf16[8,3,768]{2,1,0:T(4,128)(2,1)}), bf16[8,3,768]{2,1,0:T(4,128)(2,1)S(1)}, u32[]{:S(2)}, u32[]{:S(2)}) async-start(bf16[8,3,768]{2,1,0:T(4,128)(2,1)} %reshape.138), calls=%async_computation.5 | async-start | bytes 98304 | tf_op jit(solution)/shard_map/all_to_all | solution.py:106
  349.9 3.8 %all-to-all-done.5 = bf16[8,3,768]{2,1,0:T(4,128)(2,1)S(1)} async-done(((bf16[8,3,768]{2,1,0:T(4,128)(2,1)}), bf16[8,3,768]{2,1,0:T(4,128)(2,1)S(1)}, u32[]{:S(2)}, u32[]{:S(2)}) %all-to-all-start.5) | async-done | bytes 36896 | tf_op jit(solution)/shard_map/all_to_all | solution.py:106
  (138 shorter events, 44.2 us)
Async XLA Ops:
  7.2 62.0 %copy-start = (bf16[384,384]{1,0:T(8,128)(2,1)S(1)}, bf16[384,384]{1,0:T(8,128)(2,1)}, u32[]{:S(2)}) copy-start(bf16[384,384]{1,0:T(8,128)(2,1)} %param.14) | copy-start | bytes 884740
  10.2 59.3 %copy-start.17 = (f32[112,56]{1,0:T(8,128)}, f32[112,56]{1,0:T(8,128)S(1)}, u32[]{:S(2)}) copy-start(f32[112,56]{1,0:T(8,128)S(1)} %broadcast_multiply_fusion.2) | copy-start | bytes 75268
  10.3 56.9 %copy-start.3 = (bf16[384,384]{1,0:T(8,128)(2,1)S(1)}, bf16[384,384]{1,0:T(8,128)(2,1)}, u32[]{:S(2)}) copy-start(bf16[384,384]{1,0:T(8,128)(2,1)} %param.15) | copy-start | bytes 884740
  13.3 56.3 %copy-start.1 = (bf16[112,56,128]{2,1,0:T(8,128)(2,1)S(1)}, bf16[112,56,128]{2,1,0:T(8,128)(2,1)}, u32[]{:S(2)}) copy-start(bf16[112,56,128]{2,1,0:T(8,128)(2,1)} %param.10) | copy-start | bytes 4816900
  13.3 56.2 %copy-start.28 = (f32[128]{0:T(128)S(1)}, f32[128]{0:T(128)}, u32[]{:S(2)}) copy-start(f32[128]{0:T(128)} %param.11) | copy-start | bytes 1540
  13.3 56.2 %copy-start.29 = (bf16[128,16]{0,1:T(8,128)(2,1)S(1)}, bf16[128,16]{0,1:T(8,128)(2,1)}, u32[]{:S(2)}) copy-start(bf16[128,16]{0,1:T(8,128)(2,1)} %param.12) | copy-start | bytes 12292
  13.4 59.5 %copy-start.22 = (f32[112,56]{1,0:T(8,128)}, f32[112,56]{1,0:T(8,128)S(1)}, u32[]{:S(2)}) copy-start(f32[112,56]{1,0:T(8,128)S(1)} %add_rsqrt_fusion) | copy-start | bytes 75268
  74.5 22.9 %copy-start.27 = (bf16[7,384]{1,0:T(8,128)(2,1)S(1)}, bf16[7,384]{1,0:T(8,128)(2,1)}, u32[]{:S(2)}) copy-start(bf16[7,384]{1,0:T(8,128)(2,1)} %param.19) | copy-start | bytes 16132
  75.7 20.5 %all-to-all-start = ((f32[16,32,112]{2,1,0:T(8,128)}), f32[16,32,112]{2,1,0:T(8,128)S(1)}, u32[]{:S(2)}, u32[]{:S(2)}) async-start(f32[16,32,112]{2,1,0:T(8,128)} %broadcast_in_dim.31), calls=%async_computation | async-start | bytes 524288 | tf_op jit(solution)/shard_map/all_to_all | solution.py:41
  82.1 80.6 %all-gather.5.cloned.1.call-start = ((), (), s32[]{:S(2)}) async-start(), calls=%async_computation.7 | async-start | bytes 2924544 | tf_op jit(solution)/shard_map/all_gather | solution.py:82
  83.3 38.7 %copy-start.24 = (bf16[56,384]{0,1:T(8,128)(2,1)}, bf16[56,384]{0,1:T(8,128)(2,1)S(1)}, u32[]{:S(2)}) copy-start(bf16[56,384]{0,1:T(8,128)(2,1)S(1)} %copy.82) | copy-start | bytes 129028
  98.0 22.2 %all-to-all-start.1 = ((bf16[16,7,384]{2,1,0:T(8,128)(2,1)}), bf16[16,7,384]{2,1,0:T(8,128)(2,1)S(1)}, u32[]{:S(2)}, u32[]{:S(2)}) async-start(bf16[16,7,384]{2,1,0:T(8,128)(2,1)} %broadcast_in_dim.32), calls=%async_computation.1 | async-start | bytes 196608 | tf_op jit(solution)/shard_map/all_to_all | solution.py:41
  122.8 43.2 %copy-start.9 = (bf16[112,384]{0,1:T(8,128)(2,1)S(1)}, bf16[112,384]{0,1:T(8,128)(2,1)}, u32[]{:S(2)}) copy-start(bf16[112,384]{0,1:T(8,128)(2,1)} %copy-done.8) | copy-start | bytes 258052
  122.8 43.5 %all-to-all-start.4 = ((bf16[8,56,384]{2,1,0:T(8,128)(2,1)}), bf16[8,56,384]{2,1,0:T(8,128)(2,1)S(1)}, u32[]{:S(2)}, u32[]{:S(2)}) async-start(bf16[8,56,384]{2,1,0:T(8,128)(2,1)} %broadcast_in_dim.35), calls=%async_computation.4 | async-start | bytes 688128 | tf_op jit(solution)/shard_map/all_to_all | solution.py:41
  164.6 33.6 %copy-start.2 = (f32[112,384]{1,0:T(8,128)}, f32[112,384]{1,0:T(8,128)S(1)}, u32[]{:S(2)}) copy-start(f32[112,384]{1,0:T(8,128)S(1)} %reduce_sum.111) | copy-start | bytes 516100
  167.1 20.7 %all-to-all-start.3 = ((bf16[8,56,384]{2,1,0:T(8,128)(2,1)}), bf16[8,56,384]{2,1,0:T(8,128)(2,1)S(1)}, u32[]{:S(2)}, u32[]{:S(2)}) async-start(bf16[8,56,384]{2,1,0:T(8,128)(2,1)} %broadcast_in_dim.34), calls=%async_computation.3 | async-start | bytes 688128 | tf_op jit(solution)/shard_map/all_to_all | solution.py:41
  180.7 29.5 %copy-start.15 = (f32[56,384]{1,0:T(8,128)}, f32[56,384]{1,0:T(8,128)S(1)}, u32[]{:S(2)}) copy-start(f32[56,384]{1,0:T(8,128)S(1)} %convert_reduce_fusion.2) | copy-start | bytes 258052
  187.9 22.3 %copy-start.13 = (f32[56,384]{1,0:T(8,128)}, f32[56,384]{1,0:T(8,128)S(1)}, u32[]{:S(2)}) copy-start(f32[56,384]{1,0:T(8,128)S(1)} %convert_reduce_fusion.3) | copy-start | bytes 258052
  189.7 19.3 %all-to-all-start.6 = ((bf16[16,3,768]{2,1,0:T(4,128)(2,1)}), bf16[16,3,768]{2,1,0:T(4,128)(2,1)S(1)}, u32[]{:S(2)}, u32[]{:S(2)}) async-start(bf16[16,3,768]{2,1,0:T(4,128)(2,1)} %reshape.139), calls=%async_computation.6 | async-start | bytes 196608 | tf_op jit(solution)/shard_map/all_to_all | solution.py:106
  210.2 120.8 %all-to-all-start.2 = ((bf16[16,112,384]{2,1,0:T(8,128)(2,1)}), bf16[16,112,384]{2,1,0:T(8,128)(2,1)S(1)}, u32[]{:S(2)}, u32[]{:S(2)}) async-start(bf16[16,112,384]{2,1,0:T(8,128)(2,1)} %broadcast_in_dim.33), calls=%async_computation.2 | async-start | bytes 2752512 | tf_op jit(solution)/shard_map/all_to_all | solution.py:41
  229.0 66.5 %copy-start.12 = (bf16[112,384]{1,0:T(8,128)(2,1)S(1)}, bf16[112,384]{1,0:T(8,128)(2,1)}, u32[]{:S(2)}) copy-start(bf16[112,384]{1,0:T(8,128)(2,1)} %copy-done.11) | copy-start | bytes 258052
  297.2 33.1 %copy-start.21 = (bf16[16,3,768]{2,1,0:T(4,128)(2,1)S(1)}, bf16[16,3,768]{2,1,0:T(4,128)(2,1)}, u32[]{:S(2)}) copy-start(bf16[16,3,768]{2,1,0:T(4,128)(2,1)} %copy-done.20) | copy-start | bytes 221188
  304.9 26.3 %copy-start.25 = (bf16[112,24]{0,1:T(8,128)(2,1)S(1)}, bf16[112,24]{0,1:T(8,128)(2,1)}, u32[]{:S(2)}) copy-start(bf16[112,24]{0,1:T(8,128)(2,1)} %reshape.136) | copy-start | bytes 16132
  332.0 21.7 %all-to-all-start.5 = ((bf16[8,3,768]{2,1,0:T(4,128)(2,1)}), bf16[8,3,768]{2,1,0:T(4,128)(2,1)S(1)}, u32[]{:S(2)}, u32[]{:S(2)}) async-start(bf16[8,3,768]{2,1,0:T(4,128)(2,1)} %reshape.138), calls=%async_computation.5 | async-start | bytes 98304 | tf_op jit(solution)/shard_map/all_to_all | solution.py:106
  (14 other events, 93.8 us)
Sparse Core Ops, SparseCore 0:
  97.5 65.1 all-gather.4
where the time goes:
time: 363 us; the launch traced here: 361 us
  blocking collectives  137 us (38%)
  waiting for transfers between devices  78.8 us (22%)
  starting transfers between devices  65.5 us (18%)
  matrix products  25.3 us (7%)
  local copies, waits for them, and re-layouts  21.3 us (6%)
  other arithmetic  18.7 us (5%)
  between operations  14.8 us (4%)
    psum x3, blocking collectives, over_axes(): return functools.reduce(lax.psum, axes, array)  60 us
    all_gather x3, blocking collectives, stacked_from(): pieces = lax.all_gather(pieces, axes[k], axis=0, tiled=True)  52.2 us
    all_to_all x5, starting transfers between devices, from_everyone(): lax.all_to_all(jnp.broadcast_to(array[None], (devices, *array.shape)), ax...  41.1 us
    all_gather x1, waiting for transfers between devices, over_pieces(): pieces = lax.all_gather(array, axis)  33.4 us
    all_to_all x5, waiting for transfers between devices, from_everyone(): lax.all_to_all(jnp.broadcast_to(array[None], (devices, *array.shape)), ax...  31 us
    all_gather x1, blocking collectives, broadcast(): lax.all_gather(array, axis)  24.5 us
    all_to_all x2, starting transfers between devices, sum_at_owner(): lax.all_to_all(split_up(array, dim, devices), axis, 0, 0, tiled=True)  24.3 us
    all_to_all x2, waiting for transfers between devices, sum_at_owner(): lax.all_to_all(split_up(array, dim, devices), axis, 0, 0, tiled=True)  14.4 us
  transfers between devices with their start and end apart: 8, of which 6 were waited for; matrix products, arithmetic and copies ran while one was open for 12% of the time, Pallas kernels for 0%

commit v1 on v0

--- a/solution.py
+++ b/solution.py
@@ -25,7 +25,10 @@
 def stacked_from(array, axes, sequence):
     pieces = array[None]
     for k in sequence:
-        pieces = lax.all_gather(pieces, axes[k], axis=0, tiled=True)
+        count = lax.axis_size(axes[k])
+        blocks = jnp.stack([pieces for _ in range(count)])
+        blocks = lax.all_to_all(blocks, axes[k], split_axis=0, concat_axis=0)
+        pieces = jnp.concatenate(blocks, axis=0)
     carried = [lax.axis_size(axes[k]) for k in reversed(sequence)]
     pieces = pieces.reshape(*carried, *array.shape)
     turned = sorted(range(len(sequence)), key=lambda place: sequence[len(sequence) - 1 - place])

time: 363 us -> 344 us (0.948)
  blocking collectives: 137 us -> 92.7 us
  starting transfers between devices: 65.5 us -> 81.2 us
  waiting for transfers between devices: 78.8 us -> 85.6 us
    all_gather x3 -> x0, blocking collectives: 52.2 us -> none  [stacked_from(): pieces = lax.all_gather(pieces, axes[k], axis=0, tiled=True)]
    all_to_all x0 -> x2, starting transfers between devices: none -> 19.7 us  [stacked_from(): blocks = lax.all_to_all(blocks, axes[k], split_axis=0, concat_axis=0)]
    all_to_all x0 -> x1, blocking collectives: none -> 8.08 us  [stacked_from(): blocks = lax.all_to_all(blocks, axes[k], split_axis=0, concat_axis=0)]
    all_to_all x0 -> x2, waiting for transfers between devices: none -> 7.53 us  [stacked_from(): blocks = lax.all_to_all(blocks, axes[k], split_axis=0, concat_axis=0)]
    all_to_all x5, starting transfers between devices: 41.1 us -> 37.2 us  [from_everyone(): lax.all_to_all(jnp.broadcast_to(array[None], (devices, *array.shape)), ax...]
  transfers between devices with their start and end apart: 8 -> 10, of which waited for: 6 -> 8; matrix products, arithmetic and copies ran while one was open for 12% -> 15% of each run, Pallas kernels for 0% -> 0%
where the time goes in v1:
time: 344 us; the launch traced here: 342 us
  blocking collectives  92.7 us (27%)
  waiting for transfers between devices  85.6 us (25%)
  starting transfers between devices  81.2 us (24%)
  matrix products  25.4 us (7%)
  local copies, waits for them, and re-layouts  24.8 us (7%)
  other arithmetic  18 us (5%)
  between operations  14.7 us (4%)
    psum x3, blocking collectives, over_axes(): return functools.reduce(lax.psum, axes, array)  60.1 us
    all_to_all x5, starting transfers between devices, from_everyone(): lax.all_to_all(jnp.broadcast_to(array[None], (devices, *array.shape)), ax...  37.2 us
    all_gather x1, waiting for transfers between devices, over_pieces(): pieces = lax.all_gather(array, axis)  33.4 us
    all_to_all x5, waiting for transfers between devices, from_everyone(): lax.all_to_all(jnp.broadcast_to(array[None], (devices, *array.shape)), ax...  30.2 us
    all_gather x1, blocking collectives, broadcast(): lax.all_gather(array, axis)  24.5 us
    all_to_all x2, starting transfers between devices, sum_at_owner(): lax.all_to_all(split_up(array, dim, devices), axis, 0, 0, tiled=True)  24.1 us
    all_to_all x2, starting transfers between devices, stacked_from(): blocks = lax.all_to_all(blocks, axes[k], split_axis=0, concat_axis=0)  19.7 us
    all_to_all x2, waiting for transfers between devices, sum_at_owner(): lax.all_to_all(split_up(array, dim, devices), axis, 0, 0, tiled=True)  14.5 us
  transfers between devices with their start and end apart: 10, of which 8 were waited for; matrix products, arithmetic and copies ran while one was open for 15% of the time, Pallas kernels for 0%

profile of v1, /device:TPU:1, one launch (start us, length us, event | category | flops | bytes accessed | tf_op | source)
XLA Modules:
  0.0 342.3 jit_solution(14451862164452213203)
XLA Ops:
  8.7 15.7 %all-to-all-start = ((bf16[16,1,7,384]{3,2,1,0:T(8,128)(2,1)}), bf16[16,1,7,384]{3,2,1,0:T(8,128)(2,1)S(1)}, u32[]{:S(2)}, u32[]{:S(2)}) async-start(bf16[16,1,7,384]{3,2,1,0:T(8,128)(2,1)} %stack.9), calls=%async_computation | async-start | bytes 196608 | tf_op jit(solution)/shard_map/all_to_all | solution.py:30
  29.8 6.5 %all-to-all-done = bf16[16,1,7,384]{3,2,1,0:T(8,128)(2,1)S(1)} async-done(((bf16[16,1,7,384]{3,2,1,0:T(8,128)(2,1)}), bf16[16,1,7,384]{3,2,1,0:T(8,128)(2,1)S(1)}, u32[]{:S(2)}, u32[]{:S(2)}) %all-to-all-start) | async-done | bytes 86048 | tf_op jit(solution)/shard_map/all_to_all | solution.py:30
  37.1 4.0 %all-to-all-start.1 = ((bf16[4,16,7,384]{3,1,2,0:T(8,128)(2,1)}), bf16[4,16,7,384]{3,1,2,0:T(8,128)(2,1)S(1)}, u32[]{:S(2)}, u32[]{:S(2)}) async-start(bf16[4,16,7,384]{3,1,2,0:T(8,128)(2,1)} %stack.10), calls=%async_computation.1 | async-start | bytes 688128 | tf_op jit(solution)/shard_map/all_to_all | solution.py:30
  47.2 8.1 %all_to_all.50 = bf16[2,64,7,384]{3,1,2,0:T(8,128)(2,1)S(1)} all-to-all(bf16[2,64,7,384]{3,1,2,0:T(8,128)(2,1)S(1)} %pad_maximum_fusion), channel_id=1, replica_groups=mesh['sample'=4,'row_0'=4,'row_1'=2,'col'=16] {'row_1'}, dimensions={0} | all-to-all | bytes 1376256 | tf_op jit(solution)/shard_map/all_to_all | solution.py:30
  61.0 3.5 %all-to-all-start.3 = ((f32[16,32,112]{2,1,0:T(8,128)}), f32[16,32,112]{2,1,0:T(8,128)S(1)}, u32[]{:S(2)}, u32[]{:S(2)}) async-start(f32[16,32,112]{2,1,0:T(8,128)} %broadcast_in_dim.28), calls=%async_computation.3 | async-start | bytes 524288 | tf_op jit(solution)/shard_map/all_to_all | solution.py:44
  65.8 12.8 %all-to-all-done.3 = f32[16,32,112]{2,1,0:T(8,128)S(1)} async-done(((f32[16,32,112]{2,1,0:T(8,128)}), f32[16,32,112]{2,1,0:T(8,128)S(1)}, u32[]{:S(2)}, u32[]{:S(2)}) %all-to-all-start.3) | async-done | bytes 229408 | tf_op jit(solution)/shard_map/all_to_all | solution.py:44
  80.5 10.2 %all-to-all-start.4 = ((bf16[16,7,384]{2,1,0:T(8,128)(2,1)}), bf16[16,7,384]{2,1,0:T(8,128)(2,1)S(1)}, u32[]{:S(2)}, u32[]{:S(2)}) async-start(bf16[16,7,384]{2,1,0:T(8,128)(2,1)} %broadcast_in_dim.29), calls=%async_computation.4 | async-start | bytes 196608 | tf_op jit(solution)/shard_map/all_to_all | solution.py:44
  90.7 11.9 %all-to-all-done.4 = bf16[16,7,384]{2,1,0:T(8,128)(2,1)S(1)} async-done(((bf16[16,7,384]{2,1,0:T(8,128)(2,1)}), bf16[16,7,384]{2,1,0:T(8,128)(2,1)S(1)}, u32[]{:S(2)}, u32[]{:S(2)}) %all-to-all-start.4) | async-done | bytes 86048 | tf_op jit(solution)/shard_map/all_to_all | solution.py:44
  105.1 6.2 %all-to-all-start.7 = ((bf16[8,56,384]{2,1,0:T(8,128)(2,1)}), bf16[8,56,384]{2,1,0:T(8,128)(2,1)S(1)}, u32[]{:S(2)}, u32[]{:S(2)}) async-start(bf16[8,56,384]{2,1,0:T(8,128)(2,1)} %broadcast_in_dim.32), calls=%async_computation.7 | async-start | bytes 688128 | tf_op jit(solution)/shard_map/all_to_all | solution.py:44
  111.3 33.4 %all-gather.3.cloned.1.call-done = f32[16,112,384]{2,1,0:T(8,128)} async-done(((f32[1,112,384]{2,1,0:T(8,128)}), f32[16,112,384]{2,1,0:T(8,128)}) %all-gather.3.cloned.1.call-update) | async-done | bytes 2752528 | tf_op jit(solution)/shard_map/all_gather | solution.py:85
  149.2 12.7 %all-to-all-start.6 = ((bf16[8,56,384]{2,1,0:T(8,128)(2,1)}), bf16[8,56,384]{2,1,0:T(8,128)(2,1)S(1)}, u32[]{:S(2)}, u32[]{:S(2)}) async-start(bf16[8,56,384]{2,1,0:T(8,128)(2,1)} %broadcast_in_dim.31), calls=%async_computation.6 | async-start | bytes 688128 | tf_op jit(solution)/shard_map/all_to_all | solution.py:44
  163.6 5.5 %all-to-all-done.6 = bf16[8,56,384]{2,1,0:T(8,128)(2,1)S(1)} async-done(((bf16[8,56,384]{2,1,0:T(8,128)(2,1)}), bf16[8,56,384]{2,1,0:T(8,128)(2,1)S(1)}, u32[]{:S(2)}, u32[]{:S(2)}) %all-to-all-start.6) | async-done | bytes 344096 | tf_op jit(solution)/shard_map/all_to_all | solution.py:44
  171.0 7.2 %all-to-all-start.9 = ((bf16[16,3,768]{2,1,0:T(4,128)(2,1)}), bf16[16,3,768]{2,1,0:T(4,128)(2,1)S(1)}, u32[]{:S(2)}, u32[]{:S(2)}) async-start(bf16[16,3,768]{2,1,0:T(4,128)(2,1)} %reshape.139), calls=%async_computation.9 | async-start | bytes 196608 | tf_op jit(solution)/shard_map/all_to_all | solution.py:109
  179.5 10.6 %all-to-all-done.9 = bf16[16,3,768]{2,1,0:T(4,128)(2,1)S(1)} async-done(((bf16[16,3,768]{2,1,0:T(4,128)(2,1)}), bf16[16,3,768]{2,1,0:T(4,128)(2,1)S(1)}, u32[]{:S(2)}, u32[]{:S(2)}) %all-to-all-start.9) | async-done | bytes 73760 | tf_op jit(solution)/shard_map/all_to_all | solution.py:109
  191.3 4.6 %all-to-all-start.5 = ((bf16[16,112,384]{2,1,0:T(8,128)(2,1)}), bf16[16,112,384]{2,1,0:T(8,128)(2,1)S(1)}, u32[]{:S(2)}, u32[]{:S(2)}) async-start(bf16[16,112,384]{2,1,0:T(8,128)(2,1)} %broadcast_in_dim.30), calls=%async_computation.5 | async-start | bytes 2752512 | tf_op jit(solution)/shard_map/all_to_all | solution.py:44
  206.3 3.8 %convolution_bitcast_fusion = f32[128,16]{0,1:T(8,128)S(1)} fusion(bf16[16,112,56]{2,0,1:T(8,128)(2,1)} %copy.99, bf16[112,56,128]{2,1,0:T(8,128)(2,1)S(1)} %copy-done.1, f32[128]{0:T(128)S(1)} %copy-done.27, f32[112,56]{1,0:T(8,128)} %copy-done.22, f32[112,56]{1,0:T(8,128)} %copy-done.17), kind=kOutput, calls=%fused_computation.41 | convolution fusion | flops 29704192 | bytes 1865216 | tf_op jit(solution)/shard_map/ijc,hij->ch/dot_general | solution.py:198
  210.1 6.4 %fusion.11 = (f32[128]{0:T(128)S(1)}, f32[112,56]{1,0:T(8,128)S(1)}, f32[112,56]{1,0:T(8,128)}, f32[112,56,128]{2,1,0:T(8,128)}) fusion(bf16[112,56,128]{2,1,0:T(8,128)(2,1)S(1)} %copy-done.1, f32[112,56]{1,0:T(8,128)S(1)} %copy-done.23, f32[112,56]{1,0:T(8,128)S(1)} %copy-done.18, f32[128]{0:T(128)} %param.11, bf16[16,112,56]{2,0,1:T(8,128)(2,1)S(1)} %copy-done.19, ...), kind=kOutput, calls=%fused_computation.13 | convolution fusion | flops 32902784 | bytes 5123072 | tf_op jit(solution)/shard_map/hij,ch->ijc/dot_general | solution.py:197
  216.5 8.1 %all-reduce.1 = (f32[128,16]{0,1:T(8,128)S(1)}, f32[128]{0:T(128)}) all-reduce(f32[128,16]{0,1:T(8,128)S(1)} %convolution_bitcast_fusion, f32[128]{0:T(128)S(1)} %get-tuple-element.8), channel_id=1, replica_groups=mesh['sample'=4,'row_0'=4,'row_1'=2,'col'=16] {'row_0'}, use_global_device_ids=true, to_apply=%region_12.13 | all-reduce | flops 2176 | bytes 17408 | tf_op jit(solution)/shard_map/psum | solution.py:90
  224.7 5.9 %all-reduce.2 = (f32[128,16]{0,1:T(8,128)S(1)}, f32[128]{0:T(128)S(1)}) all-reduce(f32[128,16]{0,1:T(8,128)S(1)} %get-tuple-element.13, f32[128]{0:T(128)} %get-tuple-element.14), channel_id=1, replica_groups=mesh['sample'=4,'row_0'=4,'row_1'=2,'col'=16] {'row_1'}, use_global_device_ids=true, to_apply=%region_13.14 | all-reduce | flops 2176 | bytes 17408 | tf_op jit(solution)/shard_map/psum | solution.py:90
  230.5 46.1 %all-reduce = (f32[128,16]{0,1:T(8,128)}, f32[128]{0:T(128)}) all-reduce(f32[128,16]{0,1:T(8,128)S(1)} %get-tuple-element.15, f32[128]{0:T(128)S(1)} %get-tuple-element.16), channel_id=1, replica_groups=mesh['sample'=4,'row_0'=4,'row_1'=2,'col'=16] {'col'}, use_global_device_ids=true, to_apply=%region_14.15 | all-reduce | flops 2176 | bytes 17408 | tf_op jit(solution)/shard_map/psum | solution.py:90
  278.3 7.7 %fusion.10 = bf16[112,56,128]{2,1,0:T(8,128)(2,1)} fusion(bf16[112,56,128]{2,1,0:T(8,128)(2,1)S(1)} %copy-done.1, f32[112,56,128]{2,1,0:T(8,128)} %get-tuple-element.31, f32[112,56]{1,0:T(8,128)S(1)} %get-tuple-element.32, f32[112,56]{1,0:T(8,128)S(1)} %get-tuple-element.33, f32[128]{0:T(128)} %param.11, f32[112,56]{1,0:T(8,128)S(1)} %copy-done.23, ...), kind=kLoop, calls=%fused_computation.12 | loop fusion | flops 7225344 | bytes 6523392 | tf_op jit(solution)/shard_map/convert_element_type | solution.py:212
  286.9 24.5 %all-gather = bf16[896,384]{1,0:T(8,128)(2,1)S(1)} all-gather(bf16[56,384]{1,0:T(8,128)(2,1)S(1)} %fusion.19), channel_id=2, replica_groups=mesh['sample'=4,'row_0'=4,'row_1'=2,'col'=16] {'col'}, dimensions={0}, use_global_device_ids=true | all-gather | bytes 731136 | tf_op jit(solution)/shard_map/all_gather | solution.py:99
  313.1 16.9 %all-to-all-start.8 = ((bf16[8,3,768]{2,1,0:T(4,128)(2,1)}), bf16[8,3,768]{2,1,0:T(4,128)(2,1)S(1)}, u32[]{:S(2)}, u32[]{:S(2)}) async-start(bf16[8,3,768]{2,1,0:T(4,128)(2,1)} %reshape.138), calls=%async_computation.8 | async-start | bytes 98304 | tf_op jit(solution)/shard_map/all_to_all | solution.py:109
  331.0 3.8 %all-to-all-done.8 = bf16[8,3,768]{2,1,0:T(4,128)(2,1)S(1)} async-done(((bf16[8,3,768]{2,1,0:T(4,128)(2,1)}), bf16[8,3,768]{2,1,0:T(4,128)(2,1)S(1)}, u32[]{:S(2)}, u32[]{:S(2)}) %all-to-all-start.8) | async-done | bytes 36896 | tf_op jit(solution)/shard_map/all_to_all | solution.py:109
  (144 shorter events, 51.4 us)
Async XLA Ops:
  7.2 52.3 %copy-start = (bf16[384,384]{1,0:T(8,128)(2,1)S(1)}, bf16[384,384]{1,0:T(8,128)(2,1)}, u32[]{:S(2)}) copy-start(bf16[384,384]{1,0:T(8,128)(2,1)} %param.14) | copy-start | bytes 884740
  7.2 33.9 %copy-start.1 = (bf16[112,56,128]{2,1,0:T(8,128)(2,1)S(1)}, bf16[112,56,128]{2,1,0:T(8,128)(2,1)}, u32[]{:S(2)}) copy-start(bf16[112,56,128]{2,1,0:T(8,128)(2,1)} %param.10) | copy-start | bytes 4816900
  7.2 33.9 %copy-start.27 = (f32[128]{0:T(128)S(1)}, f32[128]{0:T(128)}, u32[]{:S(2)}) copy-start(f32[128]{0:T(128)} %param.11) | copy-start | bytes 1540
  7.2 33.9 %copy-start.28 = (bf16[128,16]{0,1:T(8,128)(2,1)S(1)}, bf16[128,16]{0,1:T(8,128)(2,1)}, u32[]{:S(2)}) copy-start(bf16[128,16]{0,1:T(8,128)(2,1)} %param.12) | copy-start | bytes 12292
  8.7 27.6 %all-to-all-start = ((bf16[16,1,7,384]{3,2,1,0:T(8,128)(2,1)}), bf16[16,1,7,384]{3,2,1,0:T(8,128)(2,1)S(1)}, u32[]{:S(2)}, u32[]{:S(2)}) async-start(bf16[16,1,7,384]{3,2,1,0:T(8,128)(2,1)} %stack.9), calls=%async_computation | async-start | bytes 196608 | tf_op jit(solution)/shard_map/all_to_all | solution.py:30
  37.1 10.0 %all-to-all-start.1 = ((bf16[4,16,7,384]{3,1,2,0:T(8,128)(2,1)}), bf16[4,16,7,384]{3,1,2,0:T(8,128)(2,1)S(1)}, u32[]{:S(2)}, u32[]{:S(2)}) async-start(bf16[4,16,7,384]{3,1,2,0:T(8,128)(2,1)} %stack.10), calls=%async_computation.1 | async-start | bytes 688128 | tf_op jit(solution)/shard_map/all_to_all | solution.py:30
  57.9 21.1 %copy-start.7 = (bf16[56,384]{0,1:T(8,128)(2,1)}, bf16[56,384]{0,1:T(8,128)(2,1)S(1)}, u32[]{:S(2)}) copy-start(bf16[56,384]{0,1:T(8,128)(2,1)S(1)} %copy.93) | copy-start | bytes 129028
  59.8 20.0 %copy-start.8 = (bf16[112,384]{0,1:T(8,128)(2,1)}, bf16[112,384]{0,1:T(8,128)(2,1)S(1)}, u32[]{:S(2)}) copy-start(bf16[112,384]{0,1:T(8,128)(2,1)S(1)} %copy.92) | copy-start | bytes 258052
  59.8 20.0 %copy-start.26 = (bf16[7,384]{1,0:T(8,128)(2,1)S(1)}, bf16[7,384]{1,0:T(8,128)(2,1)}, u32[]{:S(2)}) copy-start(bf16[7,384]{1,0:T(8,128)(2,1)} %param.19) | copy-start | bytes 16132
  61.0 17.5 %all-to-all-start.3 = ((f32[16,32,112]{2,1,0:T(8,128)}), f32[16,32,112]{2,1,0:T(8,128)S(1)}, u32[]{:S(2)}, u32[]{:S(2)}) async-start(f32[16,32,112]{2,1,0:T(8,128)} %broadcast_in_dim.28), calls=%async_computation.3 | async-start | bytes 524288 | tf_op jit(solution)/shard_map/all_to_all | solution.py:44
  64.6 80.1 %all-gather.3.cloned.1.call-start = ((), (), s32[]{:S(2)}) async-start(), calls=%async_computation.10 | async-start | bytes 2924544 | tf_op jit(solution)/shard_map/all_gather | solution.py:85
  65.7 38.5 %copy-start.24 = (bf16[56,384]{0,1:T(8,128)(2,1)}, bf16[56,384]{0,1:T(8,128)(2,1)S(1)}, u32[]{:S(2)}) copy-start(bf16[56,384]{0,1:T(8,128)(2,1)S(1)} %copy.96) | copy-start | bytes 129028
  80.5 22.1 %all-to-all-start.4 = ((bf16[16,7,384]{2,1,0:T(8,128)(2,1)}), bf16[16,7,384]{2,1,0:T(8,128)(2,1)S(1)}, u32[]{:S(2)}, u32[]{:S(2)}) async-start(bf16[16,7,384]{2,1,0:T(8,128)(2,1)} %broadcast_in_dim.29), calls=%async_computation.4 | async-start | bytes 196608 | tf_op jit(solution)/shard_map/all_to_all | solution.py:44
  105.1 42.9 %copy-start.9 = (bf16[112,384]{0,1:T(8,128)(2,1)S(1)}, bf16[112,384]{0,1:T(8,128)(2,1)}, u32[]{:S(2)}) copy-start(bf16[112,384]{0,1:T(8,128)(2,1)} %copy-done.8) | copy-start | bytes 258052
  105.1 43.3 %all-to-all-start.7 = ((bf16[8,56,384]{2,1,0:T(8,128)(2,1)}), bf16[8,56,384]{2,1,0:T(8,128)(2,1)S(1)}, u32[]{:S(2)}, u32[]{:S(2)}) async-start(bf16[8,56,384]{2,1,0:T(8,128)(2,1)} %broadcast_in_dim.32), calls=%async_computation.7 | async-start | bytes 688128 | tf_op jit(solution)/shard_map/all_to_all | solution.py:44
  146.6 44.7 %copy-start.2 = (f32[112,384]{1,0:T(8,128)}, f32[112,384]{1,0:T(8,128)S(1)}, u32[]{:S(2)}) copy-start(f32[112,384]{1,0:T(8,128)S(1)} %reduce_sum.111) | copy-start | bytes 516100
  149.2 20.0 %all-to-all-start.6 = ((bf16[8,56,384]{2,1,0:T(8,128)(2,1)}), bf16[8,56,384]{2,1,0:T(8,128)(2,1)S(1)}, u32[]{:S(2)}, u32[]{:S(2)}) async-start(bf16[8,56,384]{2,1,0:T(8,128)(2,1)} %broadcast_in_dim.31), calls=%async_computation.6 | async-start | bytes 688128 | tf_op jit(solution)/shard_map/all_to_all | solution.py:44
  169.2 22.1 %copy-start.13 = (f32[56,384]{1,0:T(8,128)}, f32[56,384]{1,0:T(8,128)S(1)}, u32[]{:S(2)}) copy-start(f32[56,384]{1,0:T(8,128)S(1)} %convert_reduce_fusion.3) | copy-start | bytes 258052
  171.0 19.1 %all-to-all-start.9 = ((bf16[16,3,768]{2,1,0:T(4,128)(2,1)}), bf16[16,3,768]{2,1,0:T(4,128)(2,1)S(1)}, u32[]{:S(2)}, u32[]{:S(2)}) async-start(bf16[16,3,768]{2,1,0:T(4,128)(2,1)} %reshape.139), calls=%async_computation.9 | async-start | bytes 196608 | tf_op jit(solution)/shard_map/all_to_all | solution.py:109
  191.3 120.8 %all-to-all-start.5 = ((bf16[16,112,384]{2,1,0:T(8,128)(2,1)}), bf16[16,112,384]{2,1,0:T(8,128)(2,1)S(1)}, u32[]{:S(2)}, u32[]{:S(2)}) async-start(bf16[16,112,384]{2,1,0:T(8,128)(2,1)} %broadcast_in_dim.30), calls=%async_computation.5 | async-start | bytes 2752512 | tf_op jit(solution)/shard_map/all_to_all | solution.py:44
  210.1 66.5 %copy-start.12 = (bf16[112,384]{1,0:T(8,128)(2,1)S(1)}, bf16[112,384]{1,0:T(8,128)(2,1)}, u32[]{:S(2)}) copy-start(bf16[112,384]{1,0:T(8,128)(2,1)} %copy-done.11) | copy-start | bytes 258052
  278.3 33.1 %copy-start.21 = (bf16[16,3,768]{2,1,0:T(4,128)(2,1)S(1)}, bf16[16,3,768]{2,1,0:T(4,128)(2,1)}, u32[]{:S(2)}) copy-start(bf16[16,3,768]{2,1,0:T(4,128)(2,1)} %copy-done.20) | copy-start | bytes 221188
  286.0 26.3 %copy-start.25 = (bf16[112,24]{0,1:T(8,128)(2,1)S(1)}, bf16[112,24]{0,1:T(8,128)(2,1)}, u32[]{:S(2)}) copy-start(bf16[112,24]{0,1:T(8,128)(2,1)} %reshape.136) | copy-start | bytes 16132
  313.1 21.7 %all-to-all-start.8 = ((bf16[8,3,768]{2,1,0:T(4,128)(2,1)}), bf16[8,3,768]{2,1,0:T(4,128)(2,1)S(1)}, u32[]{:S(2)}, u32[]{:S(2)}) async-start(bf16[8,3,768]{2,1,0:T(4,128)(2,1)} %reshape.138), calls=%async_computation.8 | async-start | bytes 98304 | tf_op jit(solution)/shard_map/all_to_all | solution.py:109
  (16 other events, 121.0 us)
Sparse Core Ops, SparseCore 0:
  79.9 64.7 all-gather.2
